TPU v7x, 32 devices: a whole 2x2x4 slice. The times are simulated.
32 devices in a mesh: dp: 1, vocab: 32 (over z, y, x, core).
Axes of the slice: x: 2, y: 2, z: 4, core: 2. Of those that a mesh axis runs over, the one named last changes fastest.
Arguments:
- input_ids: int32 [256], P('dp'), may hold values from 0 to 63999
- target_ids: int32 [256], P('dp'), may hold values from 0 to 63999
- loss_mask: int32 [256], P('dp'), may hold values 0 or 1
- final_hidden: bfloat16 [256, 3584], P('dp'), may hold values from -5 to 5, as said below
- norm_gain: float32 [3584], replicated, may hold values from 0.25 to 1.75
- embed_cotangent: bfloat16 [256, 3584], P('dp'), may hold values from -0.059814453 to 0.059814453
- table: bfloat16 [64000, 3584], P(('dp', 'vocab')), may hold values from -0.08351914 to 0.08351914, as said below
Outputs:
- embedded: bfloat16 [256, 3584], P('dp')
- loss: float32 [], replicated
- grad_hidden: bfloat16 [256, 3584], P('dp')
- gain_grad: float32 [3584], replicated
- table_grad: bfloat16 [64000, 3584], P(('dp', 'vocab'))
Inputs may be any that keep to these rules, and one draw needn't show every extreme that they name: Every entry of table lies within -5 / sqrt(3584) and 5 / sqrt(3584). Every entry of final_hidden lies within -5 and 5.
All inputs are finite; a program needn't handle non-finite values.
Results may differ from a plain program's by a relative error of at most 0.003.
Values may be sent and summed in bfloat16 or wider, within the bound.
A program may use at most 256 MiB of HBM per device.

v0:
```python
import math

import jax
import jax.numpy as jnp
from jax import lax
from jax.sharding import PartitionSpec as P

SOFTCAP = 30


EPSILON = 1e-06


def norm_backward(upstream, widened, inv_rms, norm_gain):
    scaled_up = upstream * norm_gain
    mean_dot = jnp.mean(scaled_up * widened, axis=1, keepdims=True)
    gradient = inv_rms * scaled_up - widened * (inv_rms * inv_rms * inv_rms) * mean_dot
    gain_part = jnp.sum(upstream * widened * inv_rms, axis=0)
    return (gradient.astype(jnp.bfloat16), gain_part)


def body(input_ids, target_ids, loss_mask, final_hidden, norm_gain, embed_cotangent, table):
    row_count = table.shape[0]
    embed_scale = math.sqrt(table.shape[1])
    owner = lax.axis_index(("dp", "vocab"))
    first_row = owner * row_count
    every_id, every_target, every_mask = (
        lax.all_gather(input_ids, "dp", axis=0, tiled=True),
        lax.all_gather(target_ids, "dp", axis=0, tiled=True),
        lax.all_gather(loss_mask, "dp", axis=0, tiled=True),
    )
    token_total = every_id.shape[0]
    per_group = token_total // lax.axis_size("dp")
    share_rows = token_total // lax.axis_size(("dp", "vocab"))
    widened = final_hidden.astype(jnp.float32)
    inv_rms = lax.rsqrt(jnp.mean(widened * widened, axis=1, keepdims=True) + EPSILON)
    normed = (widened * inv_rms * norm_gain).astype(jnp.bfloat16)
    normed_all, cotangent_all = (
        lax.all_gather(normed, "dp", axis=0, tiled=True),
        lax.all_gather(embed_cotangent, "dp", axis=0, tiled=True),
    )

    def lookup_term():
        wanted = lax.slice_in_dim(every_id, 0, per_group * lax.axis_size("dp"), axis=0) - first_row
        inside = (wanted >= 0) & (wanted < row_count)
        picked = jnp.take(table, jnp.clip(wanted, 0, row_count - 1), axis=0)
        return jnp.where(inside[:, None], picked.astype(jnp.float32), 0.0)

    group_rows = lax.psum_scatter(
        lookup_term().astype(jnp.bfloat16), "dp", scatter_dimension=0, tiled=True
    ).astype(jnp.float32)
    found = lax.psum(group_rows.astype(jnp.bfloat16), "vocab").astype(jnp.float32)
    embedded = (found * embed_scale).astype(jnp.bfloat16)
    raw_logits = lax.dot_general(
        normed_all, table, (((1,), (1,)), ((), ())), preferred_element_type=jnp.float32
    )
    capped = SOFTCAP * jnp.tanh(raw_logits / SOFTCAP)
    exp_logits = jnp.exp(capped)
    local_targets = every_target - first_row
    target_hit = lax.broadcasted_iota(jnp.int32, capped.shape, 1) == local_targets[:, None]
    token_weight = every_mask.astype(jnp.float32)
    picked_sum = jnp.sum(token_weight * jnp.sum(jnp.where(target_hit, capped, 0.0), axis=1))
    sum_exp, target_sum = lax.psum((jnp.sum(exp_logits, axis=1), picked_sum), ("dp", "vocab"))
    loss = (jnp.sum(token_weight * jnp.log(sum_exp)) - target_sum) / jnp.maximum(
        jnp.sum(token_weight), 1.0
    )
    slope = (
        token_weight[:, None]
        * (exp_logits / sum_exp[:, None] - target_hit.astype(jnp.float32))
        * (1.0 - (capped / SOFTCAP) ** 2)
    )
    slope_low = slope.astype(jnp.bfloat16)
    head_part = lax.dot_general(
        slope_low, normed_all, (((0,), (0,)), ((), ())), preferred_element_type=jnp.float32
    )
    local_ids = every_id - first_row
    owned = (local_ids >= 0) & (local_ids < row_count)
    segment_ids = jnp.where(owned, local_ids, row_count)
    embed_part = (
        jax.ops.segment_sum(
            cotangent_all.astype(jnp.float32), segment_ids, num_segments=row_count + 1
        )[:row_count]
        * embed_scale
    )
    table_grad = (head_part + embed_part).astype(jnp.bfloat16)

    def upstream_term():
        block = lax.slice_in_dim(slope_low, 0, share_rows * lax.axis_size(("dp", "vocab")), axis=0)
        return jnp.dot(block, table, preferred_element_type=jnp.float32)

    upstream = lax.psum_scatter(upstream_term(), ("dp", "vocab"), scatter_dimension=0, tiled=True)
    offset_rows = lax.axis_index("vocab") * share_rows
    widened_share = lax.dynamic_slice_in_dim(widened, offset_rows, share_rows, 0)
    inv_share = lax.dynamic_slice_in_dim(inv_rms, offset_rows, share_rows, 0)
    gradient_share, gain_part = norm_backward(upstream, widened_share, inv_share, norm_gain)
    gain_grad = lax.psum(gain_part, ("dp", "vocab"))
    grad_hidden = lax.all_gather(gradient_share, "vocab", axis=0, tiled=True)
    return (embedded, loss, grad_hidden, gain_grad, table_grad)


def solution(mesh):
    placed = (
        P("dp"),
        P("dp"),
        P("dp"),
        P("dp", None),
        P(),
        P("dp", None),
        P(("dp", "vocab"), None),
    )
    return jax.shard_map(
        body,
        mesh=mesh,
        in_specs=placed,
        out_specs=(P("dp", None), P(), P("dp", None), P(), P(("dp", "vocab"), None)),
        check_vma=False,
    )
```

profile of v0, /device:TPU:0, one launch (start us, length us, event | category | flops | bytes accessed | tf_op | source)
XLA Modules:
  0.0 413.4 jit_solution(4255250760945379497)
XLA Ops:
  7.2 0.0 reduce-scatter.2.cloned.1.call-start
  7.2 1.9 multiply_reduce_fusion
  9.2 0.7 broadcast_subtract_fusion
  9.9 0.0 copy-start.4
  9.9 8.1 %select_reduce_fusion = (f32[256]{0:T(256)S(1)}, f32[256]{0:T(256)S(1)}, f32[256,2000]{0,1:T(8,128)S(1)}) fusion(s32[256]{0:T(256)S(1)} %broadcast_subtract_fusion, bf16[2000,3584]{1,0:T(8,128)(2,1)} %param.13, f32[3584]{0:T(1024)} %param.11, f32[256]{0:T(256)S(1)} %add_rsqrt_fusion, bf16[256,3584]{1,0:T(8,128)(2,1)} %param.10), kind=kOutput, calls=%fused_computation.15 | convolution fusion | flops 3676757504 | bytes 18237440 | tf_op jit(solution)/shard_map/dot_general | solution.py:54
  18.0 0.0 copy-start.1
  18.0 42.0 %psum.29 = f32[256]{0:T(256)S(1)} all-reduce(f32[256]{0:T(256)S(1)} %get-tuple-element.8), channel_id=1, replica_groups=mesh['dp'=1,'vocab'=32] {'dp','vocab'}, use_global_device_ids=true, to_apply=%region_3.4 | all-reduce | flops 256 | bytes 2048 | tf_op jit(solution)/shard_map/psum | solution.py:63
  59.9 0.0 copy-done.4
  59.9 9.4 %fusion.7 = f32[256,3584]{1,0:T(8,128)} fusion(bf16[2000,3584]{1,0:T(8,128)(2,1)} %param.13, f32[256,2000]{0,1:T(8,128)S(1)} %get-tuple-element.19, f32[256]{0:T(256)S(1)} %psum.29, f32[256]{0:T(256)S(1)} %convert_element_type.42, s32[256]{0:T(256)S(1)} %broadcast_subtract_fusion), kind=kOutput, calls=%fused_computation.34 | convolution fusion | flops 3675136000 | bytes 20057088 | tf_op jit(solution)/shard_map/dot_general | solution.py:89
  69.3 0.0 copy-done.1
  69.3 0.0 copy-start.3
  69.3 0.0 reduce-scatter.2.cloned.1.call-update
  69.3 0.0 all-reduce.3.cloned.1.call-start
  69.4 0.6 copy-done.3
  70.0 11.7 %gather_fusion = bf16[256,3584]{1,0:T(8,128)(2,1)} fusion(bf16[2000,3584]{1,0:T(8,128)(2,1)} %param.13, s32[1024]{0:T(1024)S(1)} %pad_clamp_fusion), kind=kCustom, calls=%fused_computation | custom fusion | bytes 3671040 | tf_op jit(solution)/shard_map/jit(_take)/gather | solution.py:46
  81.7 0.0 copy-start
  81.7 3.9 select_convert_fusion
  85.5 0.0 all-reduce.3.cloned.1.call-update
  85.6 0.0 copy-start.2
  85.6 0.2 all-gather.2.cloned.1.call-start
  85.8 0.0 copy-done
  85.8 2.2 convert_element_type.43
  88.0 0.1 fusion.6
  88.1 0.6 convert_reduce_fusion
  89.4 120.7 %reduce-scatter.2.cloned.1.call-done = f32[8,3584]{1,0:T(8,128)} async-done(((f32[256,3584]{1,0:T(8,128)}), f32[8,3584]{1,0:T(8,128)}) %reduce-scatter.2.cloned.1.call-update) | async-done | bytes 114704 | tf_op jit(solution)/shard_map/reduce_scatter | solution.py:91
  210.1 0.0 copy-done.2
  210.1 1.2 multiply_reduce_fusion.1
  211.3 1.7 subtract_convert_fusion
  213.0 0.0 all-gather.2.cloned.1.call-update
  213.0 17.8 %scatter_custom_fusion = f32[2001,3584]{1,0:T(8,128)} fusion(s32[256]{0:T(256)S(1)} %subtract_select_fusion, f32[]{:T(128)} %constant.21.clone.1, bf16[256,3584]{1,0:T(8,128)(2,1)} %param.12), kind=kCustom, calls=%fused_computation.5 | custom fusion | flops 1835008 | bytes 30521348 | tf_op jit(solution)/shard_map/scatter-add | solution.py:80
  230.8 17.0 %fusion.1 = bf16[2000,3584]{1,0:T(8,128)(2,1)} fusion(f32[2001,3584]{1,0:T(8,128)} %scatter_custom_fusion, f32[3584]{0:T(1024)S(1)} %copy-done.2, f32[256]{0:T(256)S(1)} %add_rsqrt_fusion, bf16[256,3584]{1,0:T(8,128)(2,1)S(1)} %copy-done, f32[256,2000]{0,1:T(8,128)} %copy-done.1, f32[256]{0:T(256)S(1)} %psum.29, f32[256]{0:T(256)S(1)} %convert_element_type.42, ...), kind=kOutput, calls=%fused_computation.4 | convolution fusion | flops 3700310016 | bytes 46909440 | tf_op jit(solution)/shard_map/dot_general | solution.py:73
  247.8 97.6 %all-reduce.3.cloned.1.call-done = bf16[256,3584]{1,0:T(8,128)(2,1)} async-done(((bf16[256,3584]{1,0:T(8,128)(2,1)}), bf16[256,3584]{1,0:T(8,128)(2,1)}) %all-reduce.3.cloned.1.call-update) | async-done | bytes 1835024 | tf_op jit(solution)/shard_map/psum | solution.py:52
  345.4 3.0 multiply_convert_fusion.1
  348.5 39.7 %all-reduce = (f32[]{:T(128)}, f32[3584]{0:T(1024)}) all-reduce(f32[]{:T(128)} %get-tuple-element.11, f32[3584]{0:T(1024)S(1)} %get-tuple-element.5), channel_id=1, replica_groups=mesh['dp'=1,'vocab'=32] {'dp','vocab'}, use_global_device_ids=true, to_apply=%region_7.8 | all-reduce | flops 3585 | bytes 28680 | tf_op jit(solution)/shard_map/psum | solution.py:63
  389.4 13.4 %all-gather.2.cloned.1.call-done = bf16[256,3584]{1,0:T(8,128)(2,1)} async-done(((bf16[8,3584]{1,0:T(8,128)(2,1)}), bf16[256,3584]{1,0:T(8,128)(2,1)}) %all-gather.2.cloned.1.call-update) | async-done | bytes 1835024 | tf_op jit(solution)/shard_map/all_gather | solution.py:97
  402.8 2.8 copy.14
  (6 shorter events, 0.0 us)
Async XLA Ops:
  7.2 203.0 %reduce-scatter.2.cloned.1.call-start = ((), (), s32[]{:S(2)}) async-start(), calls=%async_computation.2 | async-start | bytes 3784704 | tf_op jit(solution)/shard_map/reduce_scatter | solution.py:91
  9.9 50.1 %copy-start.4 = (s32[256]{0:T(256)S(1)}, s32[256]{0:T(256)}, u32[]{:S(2)}) copy-start(s32[256]{0:T(256)} %param.9) | copy-start | bytes 3076
  18.0 51.3 %copy-start.1 = (f32[256,2000]{0,1:T(8,128)}, f32[256,2000]{0,1:T(8,128)S(1)}, u32[]{:S(2)}) copy-start(f32[256,2000]{0,1:T(8,128)S(1)} %get-tuple-element.19) | copy-start | bytes 6144004
  69.3 0.7 copy-start.3
  69.3 276.1 %all-reduce.3.cloned.1.call-start = ((), (), s32[]{:S(2)}) async-start(), calls=%async_computation.1 | async-start | bytes 3670016 | tf_op jit(solution)/shard_map/psum | solution.py:52
  81.7 4.1 copy-start
  85.6 124.6 %copy-start.2 = (f32[3584]{0:T(1024)S(1)}, f32[3584]{0:T(1024)}, u32[]{:S(2)}) copy-start(f32[3584]{0:T(1024)} %param.11) | copy-start | bytes 43012
  85.6 317.3 %all-gather.2.cloned.1.call-start = ((), (), s32[]{:S(2)}) async-start(), calls=%async_computation.3 | async-start | bytes 1892352 | tf_op jit(solution)/shard_map/all_gather | solution.py:97
Sparse Core Ops, SparseCore 0:
  69.4 140.6 reduce-scatter.1
  216.0 129.3 all-reduce.2
  348.3 54.5 all-gather.1
where the time goes:
time: 414 us; the launch traced here: 413 us
  waiting for transfers between devices  232 us (56%)
  blocking collectives  81.6 us (20%)
  matrix products  34.5 us (8%)
  other arithmetic  33.1 us (8%)
  between operations  16.9 us (4%)
  local copies, waits for them, and re-layouts  15.1 us (4%)
    reduce_scatter x1, waiting for transfers between devices, body(): lax.psum_scatter(upstream_term(), ('dp', 'vocab'), scatter_dimension=0, t...  121 us
    psum x1, waiting for transfers between devices, body(): lax.psum(group_rows.astype(jnp.bfloat16), 'vocab').astype(jnp.float32)  97.6 us
    psum x2, blocking collectives, body(): lax.psum((jnp.sum(exp_logits, axis=1), picked_sum), ('dp', 'vocab'))  81.6 us
    scatter-add x1, other arithmetic, body(): jax.ops.segment_sum(cotangent_all.astype(jnp.float32), segment_ids, num_s...  17.8 us
    dot_general x1, matrix products, body(): lax.dot_general(slope_low, normed_all, (((0,), (0,)), ((), ())), preferre...  17 us
    all_gather x1, waiting for transfers between devices, body(): grad_hidden = lax.all_gather(gradient_share, 'vocab', axis=0, tiled=True)  13.4 us
    gather x1, local copies, waits for them, and re-layouts, lookup_term(): picked = jnp.take(table, jnp.clip(wanted, 0, row_count - 1), axis=0)  11.7 us
    dot_general x1, matrix products, upstream_term(): return jnp.dot(block, table, preferred_element_type=jnp.float32)  9.37 us
  transfers between devices with their start and end apart: 3, of which 3 were waited for; matrix products, arithmetic and copies ran while one was open for 14% of the time, Pallas kernels for 0%

commit v1 on v0

v1 whole, which is shorter than its diff:
```python
import functools
import math

import jax
import jax.numpy as jnp
from jax import lax
from jax.experimental import pallas as pl
from jax.experimental.pallas import tpu as pltpu
from jax.sharding import PartitionSpec as P

SOFTCAP = 30
EPSILON = 1e-06
LANES = 128


def enter(count, others):
    barrier = pltpu.get_barrier_semaphore()
    for other in others:
        pl.semaphore_signal(barrier, inc=1, device_id={"vocab": other})
    pl.semaphore_wait(barrier, count)


def stats_kernel(n, x_ref, out_ref, slots, mine, send_sem, recv_sem):
    me = lax.axis_index("vocab")
    enter(n - 1, [lax.rem(me + o, n) for o in range(1, n)])
    mine[...] = x_ref[...]

    def copy(o):
        return pltpu.make_async_remote_copy(
            src_ref=mine,
            dst_ref=slots.at[me],
            send_sem=send_sem.at[o],
            recv_sem=recv_sem.at[o],
            device_id={"vocab": lax.rem(me + o, n)},
        )

    def arrival(o):
        return pltpu.make_async_remote_copy(
            src_ref=mine,
            dst_ref=slots.at[lax.rem(me - o + n, n)],
            send_sem=send_sem.at[o],
            recv_sem=recv_sem.at[o],
            device_id={"vocab": lax.rem(me + o, n)},
        )

    for o in range(1, n):
        copy(o).start()
    slots[me] = x_ref[...]
    for o in range(1, n):
        arrival(o).wait_recv()
    total = slots[0]
    for source in range(1, n):
        total = total + slots[source]
    out_ref[...] = total
    for o in range(1, n):
        copy(o).wait_send()


def exchange_stats(n, values):
    if n == 1:
        return values
    return pl.pallas_call(
        functools.partial(stats_kernel, n),
        out_shape=jax.ShapeDtypeStruct(values.shape, values.dtype),
        in_specs=[pl.BlockSpec(memory_space=pltpu.VMEM)],
        out_specs=pl.BlockSpec(memory_space=pltpu.VMEM),
        scratch_shapes=[
            pltpu.VMEM((n,) + values.shape, values.dtype),
            pltpu.VMEM(values.shape, values.dtype),
            pltpu.SemaphoreType.DMA((n,)),
            pltpu.SemaphoreType.DMA((n,)),
        ],
        compiler_params=pltpu.CompilerParams(collective_id=1, has_side_effects=True),
    )(values)


def stream_plan(levels, width):
    rest = [g for g in ([1], [2], list(range(3, levels))) if g and g[-1] < levels]
    shares = [11, 10, 7]
    tiles = width // LANES
    plans, start = [], 0
    for i in range(max(1, len(rest))):
        order = [0] + [b for g in rest[i:] + rest[:i] for b in g]
        last = i == max(1, len(rest)) - 1
        stop = tiles if last else start + tiles * shares[i] // sum(shares)
        plans.append((slice(start * LANES, stop * LANES), order))
        start = stop
    return plans


def hidden_kernel(levels, plans, *refs):
    count = len(plans)
    up_ref, found_ref, hidden_ref, gain_ref, grad_ref, emb_ref, gain_out_ref = refs[:7]
    scratch = list(refs[7:])
    acc = [scratch.pop(0) for _ in plans]
    got_wide = [scratch.pop(0) for _ in plans]
    low = [scratch.pop(0) for _ in plans]
    got = [scratch.pop(0) for _ in plans]
    whole = [scratch.pop(0) for _ in plans]
    facc = [scratch.pop(0) for _ in plans]
    fgot = [scratch.pop(0) for _ in plans]
    fwhole = [scratch.pop(0) for _ in plans]
    gains, gain_got, send_sem, recv_sem = scratch
    n = 2**levels
    width = up_ref.shape[2]
    me = lax.axis_index("vocab")
    bits = [lax.rem(me // 2**b, 2) for b in range(levels)]
    partner = [me + (1 - 2 * bits[b]) * 2**b for b in range(levels)]
    enter(levels, partner)

    def chunk_of(position, order):
        return sum(
            lax.rem(position // 2 ** (levels - 1 - j), 2) * 2 ** order[j] for j in range(levels)
        )

    def base_of(order, known):
        return sum([bits[order[j]] * 2 ** (levels - 1 - j) for j in range(known)], 0)

    def each(size, step):
        def wrapped(i, carry):
            step(i)
            return carry

        lax.fori_loop(0, size, wrapped, 0, unroll=min(size, 4))

    def remote(src, dst, flow, stage, bit):
        return pltpu.make_async_remote_copy(
            src_ref=src,
            dst_ref=dst,
            send_sem=send_sem.at[flow, stage],
            recv_sem=recv_sem.at[flow, stage],
            device_id={"vocab": partner[bit]},
        )

    for k in range(levels):
        size = 2 ** (levels - 1 - k)
        wide = k not in (1, 2)
        sent, landed = (acc, got_wide) if wide else (low, got)
        copies = []
        for s, (columns, order) in enumerate(plans):
            bit = order[k]
            base = base_of(order, k)
            keep = base + bits[bit] * size
            give = base + (1 - bits[bit]) * size

            def prepare(i, s=s, order=order, columns=columns, give=give, keep=keep):
                if k == 0:
                    out_chunk = chunk_of(give + i, order)
                    acc[s][give + i] = up_ref[out_chunk, :, columns]
                    facc[s][give + i] = found_ref[out_chunk, :, columns].astype(jnp.bfloat16)
                elif not wide:
                    low[s][give + i] = acc[s][give + i].astype(jnp.bfloat16)

            each(size, prepare)
            arrived = pl.ds(size, size)
            first = remote(
                sent[s].at[pl.ds(give, size)], landed[s].at[arrived], s, k, bit
            )
            second = remote(
                facc[s].at[pl.ds(give, size)], fgot[s].at[arrived], count + s, k, bit
            )
            first.start()
            second.start()
            copies.append((first, second, keep))
        for s, (columns, order) in enumerate(plans):
            first, second, keep = copies[s]
            first.wait_recv()

            def add(i, s=s, order=order, columns=columns, keep=keep, landed=landed):
                arrived = landed[s][size + i].astype(jnp.float32)
                if k == 0:
                    acc[s][keep + i] = up_ref[chunk_of(keep + i, order), :, columns] + arrived
                else:
                    acc[s][keep + i] = acc[s][keep + i] + arrived

            each(size, add)
            second.wait_recv()

            def merge(i, s=s, order=order, columns=columns, keep=keep):
                arrived = fgot[s][size + i]
                if k == 0:
                    own = found_ref[chunk_of(keep + i, order), :, columns].astype(jnp.bfloat16)
                else:
                    own = facc[s][keep + i]
                facc[s][keep + i] = own + arrived

            each(size, merge)
        for first, second, _ in copies:
            first.wait_send()
            second.wait_send()

    full = hidden_ref[...]
    inv = lax.rsqrt(jnp.sum(full * full, axis=1, keepdims=True) / width + EPSILON)
    own = [base_of(order, levels) for _, order in plans]
    dot = sum(
        jnp.sum(
            acc[s][own[s]] * gain_ref[:, columns] * full[:, columns], axis=1, keepdims=True
        )
        for s, (columns, _) in enumerate(plans)
    )
    mean_dot = dot / width
    gains[0] = jnp.zeros(gains.shape[1:], jnp.float32)
    for s, (columns, _) in enumerate(plans):
        upstream = acc[s][own[s]]
        wide = full[:, columns]
        gradient = inv * (upstream * gain_ref[:, columns]) - wide * (inv * inv * inv) * mean_dot
        whole[s][own[s]] = gradient.astype(jnp.bfloat16)
        fwhole[s][own[s]] = facc[s][own[s]]
        part = jnp.sum(upstream * wide * inv, axis=0, keepdims=True)
        for j in range(columns.start // LANES, columns.stop // LANES):
            lanes = slice(j * LANES - columns.start, (j + 1) * LANES - columns.start)
            gains[0, j : j + 1, :] = part[:, lanes]

    for t in range(levels):
        size = 2**t
        stage = levels + t
        copies = []
        for s, (columns, order) in enumerate(plans):
            bit = order[levels - 1 - t]
            base = base_of(order, levels - t)
            block = pl.ds(base, size)
            copies.append(remote(whole[s].at[block], whole[s].at[block], s, stage, bit))
            copies.append(
                remote(fwhole[s].at[block], fwhole[s].at[block], count + s, stage, bit)
            )
        copies.append(remote(gains.at[t], gain_got.at[t], 2 * count, stage, t))
        for copy in copies:
            copy.start()
        for copy in copies:
            copy.wait_recv()
        gains[t + 1] = gains[t] + gain_got[t]
        for copy in copies:
            copy.wait_send()
    gain_out_ref[...] = gains[levels]
    for s, (columns, order) in enumerate(plans):

        def place(i, s=s, order=order, columns=columns):
            pair = chunk_of(i, order) // 2
            for out_ref, source in ((grad_ref, whole[s]), (emb_ref, fwhole[s])):
                both = [source[p].astype(jnp.float32) for p in (i, i + n // 2)]
                out_ref[pair, :, columns] = jnp.concatenate(both, axis=0).astype(jnp.bfloat16)

        each(n // 2, place)


def reduce_hidden(n, upstream, found, final_hidden, norm_gain):
    tokens, width = upstream.shape
    levels = n.bit_length() - 1
    share = tokens // n
    plans = stream_plan(levels, width)
    sizes = [(n, share, columns.stop - columns.start) for columns, _ in plans]
    narrow = [pltpu.VMEM((n + 1,) + size[1:], jnp.bfloat16) for size in sizes]
    first = lax.axis_index("vocab") * share
    own_hidden = lax.dynamic_slice_in_dim(final_hidden, first, share, 0).astype(jnp.float32)
    lines = -(-width // (8 * LANES)) * 8
    pairs = (n // 2, 2 * share, width)
    blocks = (n, share, width)
    flows = 2 * len(plans) + 1
    vmem = pl.BlockSpec(memory_space=pltpu.VMEM)
    grad, emb, gain = pl.pallas_call(
        functools.partial(hidden_kernel, levels, plans),
        out_shape=(
            jax.ShapeDtypeStruct(pairs, jnp.bfloat16),
            jax.ShapeDtypeStruct(pairs, jnp.bfloat16),
            jax.ShapeDtypeStruct((lines, LANES), jnp.float32),
        ),
        in_specs=[vmem] * 4,
        out_specs=(vmem, vmem, vmem),
        scratch_shapes=[pltpu.VMEM(size, jnp.float32) for size in sizes] * 2
        + narrow * 6
        + [
            pltpu.VMEM((levels + 1, lines, LANES), jnp.float32),
            pltpu.VMEM((levels, lines, LANES), jnp.float32),
            pltpu.SemaphoreType.DMA((flows, 2 * levels)),
            pltpu.SemaphoreType.DMA((flows, 2 * levels)),
        ],
        compiler_params=pltpu.CompilerParams(
            collective_id=2, has_side_effects=True, vmem_limit_bytes=48 * 1024 * 1024
        ),
    )(
        upstream.reshape(blocks),
        found.reshape(blocks),
        own_hidden,
        jnp.broadcast_to(norm_gain, (share, width)),
    )
    return grad.reshape(tokens, width), emb.reshape(tokens, width), gain.reshape(-1)[:width]


def table_kernel(scale, step, ids_ref, slope_ref, normed_ref, cotangent_ref, out_ref):
    rows, tokens = slope_ref.shape
    row_ids = lax.broadcasted_iota(jnp.int32, (rows, tokens), 0) + pl.program_id(0) * rows
    hit = (row_ids == ids_ref[...]).astype(jnp.float32).astype(jnp.bfloat16)

    def tile(j, carry):
        columns = pl.ds(pl.multiple_of(j * step, step), step)
        head = jnp.dot(
            slope_ref[...], normed_ref[:, columns], preferred_element_type=jnp.float32
        )
        embed = jnp.dot(hit, cotangent_ref[:, columns], preferred_element_type=jnp.float32)
        out_ref[:, columns] = (head + embed * scale).astype(jnp.bfloat16)
        return carry

    lax.fori_loop(0, out_ref.shape[1] // step, tile, 0)


def table_gradient(scale, local_ids, slope, normed, cotangent):
    row_count, tokens = slope.shape
    width = normed.shape[1]
    block = max(b for b in range(16, 401, 16) if row_count % b == 0)
    step = 512 if width % 512 == 0 else LANES
    vmem = pl.BlockSpec(memory_space=pltpu.VMEM)
    return pl.pallas_call(
        functools.partial(table_kernel, scale, step),
        grid=(row_count // block,),
        out_shape=jax.ShapeDtypeStruct((row_count, width), jnp.bfloat16),
        in_specs=[vmem, pl.BlockSpec((block, tokens), lambda i: (i, 0)), vmem, vmem],
        out_specs=pl.BlockSpec((block, width), lambda i: (i, 0)),
        compiler_params=pltpu.CompilerParams(vmem_limit_bytes=48 * 1024 * 1024),
        cost_estimate=pl.CostEstimate(
            flops=4 * row_count * tokens * width,
            bytes_accessed=2 * row_count * width,
            transcendentals=0,
        ),
    )(local_ids.reshape(1, tokens), slope, normed, cotangent)


def body(input_ids, target_ids, loss_mask, final_hidden, norm_gain, embed_cotangent, table):
    row_count, width = table.shape
    embed_scale = math.sqrt(width)
    n = lax.axis_size("vocab")
    first_row = lax.axis_index(("dp", "vocab")) * row_count
    every_id, every_target, every_mask = (
        lax.all_gather(a, "dp", axis=0, tiled=True) for a in (input_ids, target_ids, loss_mask)
    )
    tokens = every_id.shape[0]
    widened = final_hidden.astype(jnp.float32)
    inv_rms = lax.rsqrt(jnp.mean(widened * widened, axis=1, keepdims=True) + EPSILON)
    normed = (widened * inv_rms * norm_gain).astype(jnp.bfloat16)
    normed_all, cotangent_all = (
        lax.all_gather(a, "dp", axis=0, tiled=True) for a in (normed, embed_cotangent)
    )
    raw_logits = lax.dot_general(
        table, normed_all, (((1,), (1,)), ((), ())), preferred_element_type=jnp.float32
    )
    capped = SOFTCAP * jnp.tanh(raw_logits / SOFTCAP)
    row_ids = lax.broadcasted_iota(jnp.int32, capped.shape, 0) + first_row
    target_hit = row_ids == every_target[None, :]
    token_weight = every_mask.astype(jnp.float32)
    sums = jnp.stack(
        [jnp.sum(jnp.exp(capped), axis=0), jnp.sum(jnp.where(target_hit, capped, 0.0), axis=0)]
    )
    sums = exchange_stats(n, sums.reshape(-1, LANES)).reshape(2, tokens)
    sum_exp, target_logit = lax.psum(sums, "dp")
    loss = jnp.sum(token_weight * (jnp.log(sum_exp) - target_logit)) / jnp.maximum(
        jnp.sum(token_weight), 1.0
    )
    slope = (
        token_weight[None, :]
        * (jnp.exp(capped) / sum_exp[None, :] - target_hit.astype(jnp.float32))
        * (1.0 - (capped / SOFTCAP) ** 2)
    ).astype(jnp.bfloat16)
    slope = lax.optimization_barrier(slope)
    id_rows = lax.broadcasted_iota(jnp.int32, (tokens, row_count), 1) + first_row
    id_hit = lax.optimization_barrier((id_rows == every_id[:, None]).astype(jnp.bfloat16))
    upstream = lax.dot_general(
        slope, table, (((0,), (0,)), ((), ())), preferred_element_type=jnp.float32
    )
    found = lax.dot_general(
        id_hit, table, (((1,), (0,)), ((), ())), preferred_element_type=jnp.float32
    )
    if lax.axis_size("dp") > 1:
        upstream = lax.psum_scatter(upstream, "dp", scatter_dimension=0, tiled=True)
        found = lax.psum_scatter(found.astype(jnp.bfloat16), "dp", scatter_dimension=0, tiled=True).astype(jnp.float32)
    grad_hidden, rows, gain_part = reduce_hidden(n, upstream, found, final_hidden, norm_gain)
    embedded = (rows.astype(jnp.float32) * embed_scale).astype(jnp.bfloat16)
    gain_grad = lax.psum(gain_part, "dp")
    table_grad = table_gradient(
        embed_scale, every_id - first_row, slope, normed_all, cotangent_all
    )
    return (embedded, loss, grad_hidden, gain_grad, table_grad)


def solution(mesh):
    placed = (
        P("dp"),
        P("dp"),
        P("dp"),
        P("dp", None),
        P(),
        P("dp", None),
        P(("dp", "vocab"), None),
    )
    return jax.shard_map(
        body,
        mesh=mesh,
        in_specs=placed,
        out_specs=(P("dp", None), P(), P("dp", None), P(), P(("dp", "vocab"), None)),
        check_vma=False,
    )
```

time: 414 us -> 149 us (0.36)
  waiting for transfers between devices: 232 us -> 0 us
  Pallas kernels: 0 us -> 100 us
  blocking collectives: 81.6 us -> 0 us
  other arithmetic: 33.1 us -> 10.5 us
  between operations: 16.9 us -> 3.2 us
  local copies, waits for them, and re-layouts: 15.1 us -> 3.37 us
    reduce_scatter x1 -> x0, waiting for transfers between devices: 121 us -> none  [body(): lax.psum_scatter(upstream_term(), ('dp', 'vocab'), scatter_dimension=0, t...]
    pallas_call x0 -> x3, Pallas kernels: none -> 100 us  [the longest x1 73 us: reduce_hidden(): pl.pallas_call(functools.partial(hidden_kernel, levels, plans), out_shape...]
    psum x1 -> x0, waiting for transfers between devices: 97.6 us -> none  [body(): lax.psum(group_rows.astype(jnp.bfloat16), 'vocab').astype(jnp.float32)]
    psum x2 -> x0, blocking collectives: 81.6 us -> none  [body(): lax.psum((jnp.sum(exp_logits, axis=1), picked_sum), ('dp', 'vocab'))]
    scatter-add x1 -> x0, other arithmetic: 17.8 us -> none  [body(): jax.ops.segment_sum(cotangent_all.astype(jnp.float32), segment_ids, num_s...]
    all_gather x1 -> x0, waiting for transfers between devices: 13.4 us -> none  [body(): grad_hidden = lax.all_gather(gradient_share, 'vocab', axis=0, tiled=True)]
    gather x1 -> x0, local copies, waits for them, and re-layouts: 11.7 us -> none  [lookup_term(): picked = jnp.take(table, jnp.clip(wanted, 0, row_count - 1), axis=0)]
    convert_element_type x4 -> x5, other arithmetic: 10.8 us -> 6.43 us  [the longest x1 2.29 us: body(): slope = (token_weight[None, :] * (jnp.exp(capped) / sum_exp[None, :] - ta...]
  transfers between devices with their start and end apart: 3 -> 0, of which waited for: 3 -> 0; matrix products, arithmetic and copies ran while one was open for 14% -> 0% of each run, Pallas kernels for 0% -> 0%
where the time goes in v1:
time: 149 us; the launch traced here: 148 us
  Pallas kernels  100 us (67%)
  matrix products  31.1 us (21%)
  other arithmetic  10.5 us (7%)
  local copies, waits for them, and re-layouts  3.37 us (2%)
  between operations  3.2 us (2%)
    pallas_call x1, Pallas kernels, reduce_hidden(): pl.pallas_call(functools.partial(hidden_kernel, levels, plans), out_shape...  73 us
    pallas_call x1, Pallas kernels, table_gradient(): pl.pallas_call(functools.partial(table_kernel, scale, step), grid=(row_co...  15.4 us
    pallas_call x1, Pallas kernels, exchange_stats(): pl.pallas_call(functools.partial(stats_kernel, n), out_shape=jax.ShapeDty...  11.7 us
    dot_general x1, matrix products, body(): lax.dot_general(id_hit, table, (((1,), (0,)), ((), ())), preferred_elemen...  11.2 us
    dot_general x1, matrix products, body(): lax.dot_general(table, normed_all, (((1,), (1,)), ((), ())), preferred_el...  10.9 us
    dot_general x1, matrix products, body(): lax.dot_general(slope, table, (((0,), (0,)), ((), ())), preferred_element...  9.1 us

profile of v1, /device:TPU:0, one launch (start us, length us, event | category | flops | bytes accessed | tf_op | source)
XLA Modules:
  0.0 148.3 jit_solution(1059189251387739364)
XLA Ops:
  0.6 0.0 copy-start.2
  0.6 0.0 copy-start.4
  0.7 0.0 copy-start.1
  0.7 0.8 broadcast_subtract_fusion
  1.5 0.7 convert_element_type.31
  2.2 1.9 %fusion = f32[256]{0:T(256)S(1)} fusion(bf16[256,3584]{1,0:T(8,128)(2,1)} %param.10), kind=kLoop, calls=%fused_computation.4 | loop fusion | flops 2752256 | bytes 1836032 | tf_op jit(solution)/shard_map/reduce_sum | solution.py:337
  4.1 0.8 dynamic-slice_convert_fusion.refs_2_
  5.0 0.0 copy-done.2
  5.0 0.0 copy-done.4
  5.0 1.2 compare_convert_fusion.1
  6.2 0.0 copy-done.1
  6.2 0.0 copy-start.6
  6.2 0.5 fusion.2.normed_ref
  6.7 0.2 copy-done.6
  6.9 10.9 %fusion.9 = (f32[256]{0:T(256)S(1)}, f32[256]{0:T(256)S(1)}, f32[256,2000]{0,1:T(8,128)}) fusion(s32[256]{0:T(256)S(1)} %copy-done.6, s32[2000]{0:T(1024)S(1)} %iota_add_fusion, bf16[256,3584]{1,0:T(8,128)(2,1)S(1)} %fusion.2.normed_ref, bf16[2000,3584]{1,0:T(8,128)(2,1)} %param.13), kind=kOutput, calls=%fused_computation.19 | convolution fusion | flops 3673087488 | bytes 18230080 | tf_op jit(solution)/shard_map/dot_general | solution.py:342
  17.7 0.0 copy-start.5
  17.8 0.6 reshape.50.x_ref
  18.4 11.7 %shard_map.110 = f32[4,128]{1,0:T(4,128)} custom-call(f32[4,128]{1,0:T(4,128)} %reshape.50.x_ref), custom_call_target="tpu_custom_call" | custom-call | tf_op jit(solution)/shard_map/pallas_call | solution.py:62
  30.1 0.0 copy-start.3
  30.1 0.7 slice_bitcast_fusion.1
  30.9 2.3 %fusion.8.slope_ref = bf16[2000,256]{1,0:T(8,128)(2,1)S(1)} fusion(f32[256,2000]{0,1:T(8,128)} %get-tuple-element.15, f32[256]{0:T(256)S(1)} %slice_bitcast_fusion.1, s32[256]{0:T(256)S(1)} %copy-done.6, f32[256]{0:T(256)S(1)} %convert_element_type.31, s32[2000]{0:T(1024)S(1)} %iota_add_fusion), kind=kLoop, calls=%fused_computation.17 | loop fusion | flops 5120000 | bytes 3083072 | tf_op jit(solution)/shard_map/convert_element_type | solution.py:361
  33.2 0.0 copy-done.5
  33.2 0.0 copy-done.3
  33.2 0.6 convert_reduce_fusion
  35.1 11.2 %convolution_bitcast_fusion.refs_1_ = f32[32,8,3584]{2,1,0:T(8,128)} fusion(bf16[256,2000]{1,0:T(8,128)(2,1)} %compare_convert_fusion.1, bf16[2000,3584]{1,0:T(8,128)(2,1)} %param.13), kind=kOutput, calls=%fused_computation | convolution fusion | flops 3670016000 | bytes 19030016 | tf_op jit(solution)/shard_map/dot_general | solution.py:368
  46.3 9.1 %convolution_bitcast_fusion.1.refs_0_ = f32[32,8,3584]{2,1,0:T(8,128)} fusion(bf16[2000,256]{1,0:T(8,128)(2,1)S(1)} %fusion.8.slope_ref, bf16[2000,3584]{1,0:T(8,128)(2,1)} %param.13), kind=kOutput, calls=%fused_computation.1 | convolution fusion | flops 3670016000 | bytes 19030016 | tf_op jit(solution)/shard_map/dot_general | solution.py:365
  55.4 73.0 %shard_map.111 = (bf16[16,16,3584]{2,1,0:T(8,128)(2,1)S(1)}, bf16[16,16,3584]{2,1,0:T(8,128)(2,1)S(1)}, f32[32,128]{1,0:T(8,128)S(1)}) custom-call(f32[32,8,3584]{2,1,0:T(8,128)} %convolution_bitcast_fusion.1.refs_0_, f32[32,8,3584]{2,1,0:T(8,128)} %convolution_bitcast_fusion.refs_1_, f32[8,3584]{1,0:T(8,128)S(1)} %dynamic-slice_convert_fusion.refs_2_, ...), custom_call_target="tpu_custom_call" | custom-call | tf_op jit(solution)/shard_map/pallas_call | solution.py:260
  128.3 0.0 copy-start
  128.3 1.6 %multiply_convert_fusion = bf16[16,16,3584]{2,1,0:T(8,128)(2,1)} fusion(bf16[16,16,3584]{2,1,0:T(8,128)(2,1)S(1)} %get-tuple-element.8), kind=kLoop, calls=%fused_computation.7 | loop fusion | flops 2752512 | bytes 3670016 | tf_op jit(solution)/shard_map/convert_element_type | solution.py:375
  129.9 0.6 slice_bitcast_fusion
  130.5 0.0 copy-done
  130.5 15.4 %shard_map.112 = bf16[2000,3584]{1,0:T(8,128)(2,1)} custom-call(s32[1,256]{1,0:T(1,128)S(1)} %bitcast.37, bf16[2000,256]{1,0:T(8,128)(2,1)S(1)} %fusion.8.slope_ref, bf16[256,3584]{1,0:T(8,128)(2,1)S(1)} %fusion.2.normed_ref, bf16[256,3584]{1,0:T(8,128)(2,1)S(1)} %copy-done), custom_call_target="tpu_custom_call" | custom-call | flops 7340032000 | bytes 14336000 | tf_op jit(solution)/shard_map/pallas_call | solution.py:312
  145.9 1.2 copy.13
  (4 shorter events, 0.0 us)
Async XLA Ops:
  0.6 4.3 %copy-start.2 = (f32[3584]{0:T(1024)S(1)}, f32[3584]{0:T(1024)}, u32[]{:S(2)}) copy-start(f32[3584]{0:T(1024)} %param.11) | copy-start | bytes 43012
  0.6 4.4 %copy-start.4 = (s32[256]{0:T(256)S(1)}, s32[256]{0:T(256)}, u32[]{:S(2)}) copy-start(s32[256]{0:T(256)} %param.7) | copy-start | bytes 3076
  0.7 5.6 %copy-start.1 = (bf16[256,3584]{1,0:T(8,128)(2,1)S(1)}, bf16[256,3584]{1,0:T(8,128)(2,1)}, u32[]{:S(2)}) copy-start(bf16[256,3584]{1,0:T(8,128)(2,1)} %param.10) | copy-start | bytes 5505028
  6.2 0.7 copy-start.6
  17.7 15.4 %copy-start.5 = (s32[256]{0:T(256)S(1)}, s32[256]{0:T(256)}, u32[]{:S(2)}) copy-start(s32[256]{0:T(256)} %param.9) | copy-start | bytes 3076
  30.1 3.1 %copy-start.3 = (f32[4,128]{1,0:T(4,128)S(1)}, f32[4,128]{1,0:T(4,128)}, u32[]{:S(2)}) copy-start(f32[4,128]{1,0:T(4,128)} %shard_map.110) | copy-start | bytes 6148
  128.3 2.2 %copy-start = (bf16[256,3584]{1,0:T(8,128)(2,1)S(1)}, bf16[256,3584]{1,0:T(8,128)(2,1)}, u32[]{:S(2)}) copy-start(bf16[256,3584]{1,0:T(8,128)(2,1)} %cotangent_ref) | copy-start | bytes 5505028

commit v2 on v1

--- a/solution.py
+++ b/solution.py
@@ -71,6 +71,7 @@
             pltpu.SemaphoreType.DMA((n,)),
         ],
         compiler_params=pltpu.CompilerParams(collective_id=1, has_side_effects=True),
+        cost_estimate=pl.CostEstimate(flops=0, bytes_accessed=2**25, transcendentals=0),
     )(values)
 
 
@@ -97,8 +98,6 @@
     low = [scratch.pop(0) for _ in plans]
     got = [scratch.pop(0) for _ in plans]
     whole = [scratch.pop(0) for _ in plans]
-    facc = [scratch.pop(0) for _ in plans]
-    fgot = [scratch.pop(0) for _ in plans]
     fwhole = [scratch.pop(0) for _ in plans]
     gains, gain_got, send_sem, recv_sem = scratch
     n = 2**levels
@@ -131,6 +130,16 @@
             recv_sem=recv_sem.at[flow, stage],
             device_id={"vocab": partner[bit]},
         )
+
+    def gather_copy(buffers, flow, s, t):
+        order = plans[s][1]
+        block = pl.ds(base_of(order, levels - t), 2**t)
+        bit = order[levels - 1 - t]
+        stage = levels + t
+        return remote(buffers[s].at[block], buffers[s].at[block], flow + s, stage, bit)
+
+    for s, (columns, order) in enumerate(plans):
+        fwhole[s][base_of(order, levels)] = found_ref[:, columns].astype(jnp.bfloat16)
 
     for k in range(levels):
         size = 2 ** (levels - 1 - k)
@@ -147,7 +156,6 @@
                 if k == 0:
                     out_chunk = chunk_of(give + i, order)
                     acc[s][give + i] = up_ref[out_chunk, :, columns]
-                    facc[s][give + i] = found_ref[out_chunk, :, columns].astype(jnp.bfloat16)
                 elif not wide:
                     low[s][give + i] = acc[s][give + i].astype(jnp.bfloat16)
 
@@ -156,10 +164,8 @@
             first = remote(
                 sent[s].at[pl.ds(give, size)], landed[s].at[arrived], s, k, bit
             )
-            second = remote(
-                facc[s].at[pl.ds(give, size)], fgot[s].at[arrived], count + s, k, bit
-            )
             first.start()
+            second = gather_copy(fwhole, count, s, k)
             second.start()
             copies.append((first, second, keep))
         for s, (columns, order) in enumerate(plans):
@@ -175,16 +181,6 @@
 
             each(size, add)
             second.wait_recv()
-
-            def merge(i, s=s, order=order, columns=columns, keep=keep):
-                arrived = fgot[s][size + i]
-                if k == 0:
-                    own = found_ref[chunk_of(keep + i, order), :, columns].astype(jnp.bfloat16)
-                else:
-                    own = facc[s][keep + i]
-                facc[s][keep + i] = own + arrived
-
-            each(size, merge)
         for first, second, _ in copies:
             first.wait_send()
             second.wait_send()
@@ -205,25 +201,14 @@
         wide = full[:, columns]
         gradient = inv * (upstream * gain_ref[:, columns]) - wide * (inv * inv * inv) * mean_dot
         whole[s][own[s]] = gradient.astype(jnp.bfloat16)
-        fwhole[s][own[s]] = facc[s][own[s]]
         part = jnp.sum(upstream * wide * inv, axis=0, keepdims=True)
         for j in range(columns.start // LANES, columns.stop // LANES):
             lanes = slice(j * LANES - columns.start, (j + 1) * LANES - columns.start)
             gains[0, j : j + 1, :] = part[:, lanes]
 
     for t in range(levels):
-        size = 2**t
-        stage = levels + t
-        copies = []
-        for s, (columns, order) in enumerate(plans):
-            bit = order[levels - 1 - t]
-            base = base_of(order, levels - t)
-            block = pl.ds(base, size)
-            copies.append(remote(whole[s].at[block], whole[s].at[block], s, stage, bit))
-            copies.append(
-                remote(fwhole[s].at[block], fwhole[s].at[block], count + s, stage, bit)
-            )
-        copies.append(remote(gains.at[t], gain_got.at[t], 2 * count, stage, t))
+        copies = [gather_copy(whole, 0, s, t) for s in range(count)]
+        copies.append(remote(gains.at[t], gain_got.at[t], 2 * count, levels + t, t))
         for copy in copies:
             copy.start()
         for copy in copies:
@@ -267,7 +252,7 @@
         in_specs=[vmem] * 4,
         out_specs=(vmem, vmem, vmem),
         scratch_shapes=[pltpu.VMEM(size, jnp.float32) for size in sizes] * 2
-        + narrow * 6
+        + narrow * 4
         + [
             pltpu.VMEM((levels + 1, lines, LANES), jnp.float32),
             pltpu.VMEM((levels, lines, LANES), jnp.float32),
@@ -279,11 +264,30 @@
         ),
     )(
         upstream.reshape(blocks),
-        found.reshape(blocks),
+        found,
         own_hidden,
         jnp.broadcast_to(norm_gain, (share, width)),
     )
     return grad.reshape(tokens, width), emb.reshape(tokens, width), gain.reshape(-1)[:width]
+
+
+def halving_sum(n, values):
+    me = lax.axis_index("vocab")
+    for b in range(n.bit_length() - 1):
+        bit = lax.rem(me // 2**b, 2)
+        half = values.shape[0] // 2
+        give = lax.dynamic_slice_in_dim(values, (1 - bit) * half, half, 0)
+        keep = lax.dynamic_slice_in_dim(values, bit * half, half, 0)
+        pairs = [(d, d ^ 2**b) for d in range(n)]
+        arrived = lax.ppermute(give.astype(jnp.bfloat16), "vocab", pairs)
+        values = keep.astype(jnp.float32) + arrived.astype(jnp.float32)
+    return values
+
+
+def reversed_bits(n, values):
+    levels = n.bit_length() - 1
+    split = values.reshape((2,) * levels + (values.shape[0] // n,))
+    return split.transpose(tuple(reversed(range(levels))) + (levels,)).reshape(values.shape)
 
 
 def table_kernel(scale, step, ids_ref, slope_ref, normed_ref, cotangent_ref, out_ref):
@@ -339,6 +343,17 @@
     normed_all, cotangent_all = (
         lax.all_gather(a, "dp", axis=0, tiled=True) for a in (normed, embed_cotangent)
     )
+    share = tokens // lax.axis_size("dp") // n
+    groups = every_id.reshape(-1, n * share)
+    sorted_id = jax.vmap(functools.partial(reversed_bits, n))(groups).reshape(-1)
+    id_rows = lax.broadcasted_iota(jnp.int32, (tokens, row_count), 1) + first_row
+    id_hit = lax.optimization_barrier((id_rows == sorted_id[:, None]).astype(jnp.bfloat16))
+    found = lax.dot_general(
+        id_hit, table, (((1,), (0,)), ((), ())), preferred_element_type=jnp.float32
+    ).astype(jnp.bfloat16)
+    if lax.axis_size("dp") > 1:
+        found = lax.psum_scatter(found, "dp", scatter_dimension=0, tiled=True)
+    found = halving_sum(n, found)
     raw_logits = lax.dot_general(
         table, normed_all, (((1,), (1,)), ((), ())), preferred_element_type=jnp.float32
     )
@@ -360,17 +375,11 @@
         * (1.0 - (capped / SOFTCAP) ** 2)
     ).astype(jnp.bfloat16)
     slope = lax.optimization_barrier(slope)
-    id_rows = lax.broadcasted_iota(jnp.int32, (tokens, row_count), 1) + first_row
-    id_hit = lax.optimization_barrier((id_rows == every_id[:, None]).astype(jnp.bfloat16))
     upstream = lax.dot_general(
         slope, table, (((0,), (0,)), ((), ())), preferred_element_type=jnp.float32
     )
-    found = lax.dot_general(
-        id_hit, table, (((1,), (0,)), ((), ())), preferred_element_type=jnp.float32
-    )
     if lax.axis_size("dp") > 1:
         upstream = lax.psum_scatter(upstream, "dp", scatter_dimension=0, tiled=True)
-        found = lax.psum_scatter(found.astype(jnp.bfloat16), "dp", scatter_dimension=0, tiled=True).astype(jnp.float32)
     grad_hidden, rows, gain_part = reduce_hidden(n, upstream, found, final_hidden, norm_gain)
     embedded = (rows.astype(jnp.float32) * embed_scale).astype(jnp.bfloat16)
     gain_grad = lax.psum(gain_part, "dp")

time: 149 us -> 146 us (0.980)
  Pallas kernels: 100 us -> 84.6 us
  starting transfers between devices: 0 us -> 7.03 us
  matrix products: 31.1 us -> 24.2 us
  waiting for transfers between devices: 0 us -> 6.77 us
  local copies, waits for them, and re-layouts: 3.37 us -> 9.11 us
    pallas_call x1, Pallas kernels: 73 us -> 57.8 us  [reduce_hidden(): pl.pallas_call(functools.partial(hidden_kernel, levels, plans), out_shape...]
    ppermute x0 -> x5, starting transfers between devices: none -> 7.03 us  [halving_sum(): arrived = lax.ppermute(give.astype(jnp.bfloat16), 'vocab', pairs)]
    ppermute x0 -> x5, waiting for transfers between devices: none -> 6.77 us  [halving_sum(): arrived = lax.ppermute(give.astype(jnp.bfloat16), 'vocab', pairs)]
    dot_general x1, matrix products: 10.9 us -> 5.98 us  [body(): lax.dot_general(table, normed_all, (((1,), (1,)), ((), ())), preferred_el...]
    add x0 -> x5, other arithmetic: none -> 4.07 us  [halving_sum(): values = keep.astype(jnp.float32) + arrived.astype(jnp.float32)]
    unnamed x15 -> x23, local copies, waits for them, and re-layouts: 1.41 us -> 4.47 us
    dot_general x1, matrix products: 11.2 us -> 9.17 us  [body(): lax.dot_general(id_hit, table, (((1,), (0,)), ((), ())), preferred_elemen...]
    reduce_sum x1, other arithmetic: 1.94 us -> 0.44 us  [body(): jnp.mean(widened * widened, axis=1, keepdims=True) + EPSILON]
  transfers between devices with their start and end apart: 0 -> 5, of which waited for: 0 -> 3; matrix products, arithmetic and copies ran while one was open for 0% -> 14% of each run, Pallas kernels for 0% -> 18%
where the time goes in v2:
time: 146 us
  Pallas kernels  84.6 us (58%)
  matrix products  24.2 us (17%)
  other arithmetic  10.6 us (7%)
  local copies, waits for them, and re-layouts  9.11 us (6%)
  starting transfers between devices  7.03 us (5%)
  waiting for transfers between devices  6.77 us (5%)
  between operations  3.35 us (2%)
    pallas_call x1, Pallas kernels, reduce_hidden(): pl.pallas_call(functools.partial(hidden_kernel, levels, plans), out_shape...  57.8 us
    pallas_call x1, Pallas kernels, table_gradient(): pl.pallas_call(functools.partial(table_kernel, scale, step), grid=(row_co...  15.4 us
    pallas_call x1, Pallas kernels, exchange_stats(): pl.pallas_call(functools.partial(stats_kernel, n), out_shape=jax.ShapeDty...  11.4 us
    dot_general x1, matrix products, body(): lax.dot_general(id_hit, table, (((1,), (0,)), ((), ())), preferred_elemen...  9.17 us
    dot_general x1, matrix products, body(): lax.dot_general(slope, table, (((0,), (0,)), ((), ())), preferred_element...  9.05 us
    ppermute x5, starting transfers between devices, halving_sum(): arrived = lax.ppermute(give.astype(jnp.bfloat16), 'vocab', pairs)  7.03 us
    ppermute x5, waiting for transfers between devices, halving_sum(): arrived = lax.ppermute(give.astype(jnp.bfloat16), 'vocab', pairs)  6.77 us
    dot_general x1, matrix products, body(): lax.dot_general(table, normed_all, (((1,), (1,)), ((), ())), preferred_el...  5.98 us
  transfers between devices with their start and end apart: 5, of which 3 were waited for; matrix products, arithmetic and copies ran while one was open for 14% of the time, Pallas kernels for 18%

profile of v2, /device:TPU:0, one launch (start us, length us, event | category | flops | bytes accessed | tf_op | source)
XLA Modules:
  0.0 145.7 jit_solution(171509048012951354)
XLA Ops:
  0.6 0.8 reshape_reshape.3
  1.4 0.1 eq.20
  1.5 0.2 compare_convert_fusion.1
  1.8 0.0 copy-start.1
  1.8 9.2 %convolution_convert_fusion = bf16[256,3584]{1,0:T(8,128)(2,1)S(1)} fusion(bf16[256,2000]{1,0:T(8,128)(2,1)S(1)} %compare_convert_fusion.1, bf16[2000,3584]{1,0:T(8,128)(2,1)} %param.13), kind=kOutput, calls=%fused_computation.1 | convolution fusion | flops 3670933504 | bytes 17195008 | tf_op jit(solution)/shard_map/dot_general | solution.py:351
  11.0 0.0 copy-start.5
  11.0 0.0 copy-start.2
  11.0 0.0 copy-start.6
  11.0 1.0 constant_dynamic-slice_fusion
  12.0 0.5 collective-permute-start
  12.5 1.0 copy-done.2
  13.5 0.4 fusion
  13.9 0.0 copy-start.10
  14.0 0.0 copy-done.6
  14.0 0.5 fusion.2.normed_ref
  14.5 0.0 copy-done.5
  14.5 0.0 copy-done.1
  14.5 0.1 copy-done.10
  14.6 0.0 copy-start.9
  14.6 6.0 %fusion.9 = (f32[256]{0:T(256)S(1)}, f32[256]{0:T(256)S(1)}, f32[256,2000]{0,1:T(8,128)}) fusion(s32[256]{0:T(256)S(1)} %copy-done.10, s32[2000]{0:T(1024)S(1)} %iota_add_fusion, bf16[256,3584]{1,0:T(8,128)(2,1)S(1)} %fusion.2.normed_ref, bf16[2000,3584]{1,0:T(8,128)(2,1)S(1)} %copy-done.1), kind=kOutput, calls=%fused_computation.19 | convolution fusion | flops 3673087488 | bytes 18230080 | tf_op jit(solution)/shard_map/dot_general | solution.py:357
  20.6 0.0 copy-done.9
  20.6 0.6 reshape.48.x_ref
  21.2 11.4 %shard_map.110 = f32[4,128]{1,0:T(4,128)} custom-call(f32[4,128]{1,0:T(4,128)} %reshape.48.x_ref), custom_call_target="tpu_custom_call" | custom-call | bytes 33554432 | tf_op jit(solution)/shard_map/pallas_call | solution.py:62
  32.6 0.7 slice_bitcast_fusion.1
  33.3 2.3 %fusion.8.slope_ref = bf16[2000,256]{1,0:T(8,128)(2,1)S(1)} fusion(f32[256,2000]{0,1:T(8,128)} %get-tuple-element.15, f32[256]{0:T(256)S(1)} %slice_bitcast_fusion.1, s32[256]{0:T(256)S(1)} %copy-done.10, f32[256]{0:T(256)S(1)} %convert_element_type.64, s32[2000]{0:T(1024)S(1)} %iota_add_fusion), kind=kLoop, calls=%fused_computation.17 | loop fusion | flops 5120000 | bytes 3083072 | tf_op jit(solution)/shard_map/convert_element_type | solution.py:376
  35.6 0.0 collective-permute-done
  35.6 1.7 %convert_add_fusion = f32[128,3584]{1,0:T(8,128)S(1)} fusion(bf16[128,3584]{1,0:T(8,128)(2,1)} %collective-permute-done, bf16[256,3584]{1,0:T(8,128)(2,1)} %copy-done.5, s32[]{:T(128)S(6)} %select_n.53), kind=kLoop, calls=%fused_computation.20 | loop fusion | flops 1376256 | bytes 3670020 | tf_op jit(solution)/shard_map/add | solution.py:283
  37.3 0.0 copy-start.3
  37.3 1.2 copy-done.3
  38.6 0.8 dynamic-slice_convert_fusion
  39.4 0.0 copy-start.8
  39.4 1.6 %collective-permute-start.1 = (bf16[64,3584]{1,0:T(8,128)(2,1)}, bf16[64,3584]{1,0:T(8,128)(2,1)S(1)}, u32[]{:S(2)}, u32[]{:S(2)}) collective-permute-start(bf16[64,3584]{1,0:T(8,128)(2,1)} %dynamic-slice_convert_fusion), channel_id=1, source_target_pairs={{0,2},{1,3},{2,0},{3,1},{4,6},{5,7},{6,4},{7,5},{8,10},{9,11},{10,... | collective-permute-start | bytes 1376264 | tf_op jit(solution)/shard_map/ppermute | solution.py:282
  41.0 9.0 %convolution_bitcast_fusion.refs_0_ = f32[32,8,3584]{2,1,0:T(8,128)} fusion(bf16[2000,256]{1,0:T(8,128)(2,1)S(1)} %fusion.8.slope_ref, bf16[2000,3584]{1,0:T(8,128)(2,1)} %param.13), kind=kOutput, calls=%fused_computation | convolution fusion | flops 3670016000 | bytes 19030016 | tf_op jit(solution)/shard_map/dot_general | solution.py:378
  50.0 0.0 copy-done.8
  50.0 0.0 copy-start
  50.1 2.1 %collective-permute-done.1 = bf16[64,3584]{1,0:T(8,128)(2,1)S(1)} collective-permute-done((bf16[64,3584]{1,0:T(8,128)(2,1)}, bf16[64,3584]{1,0:T(8,128)(2,1)S(1)}, u32[]{:S(2)}, u32[]{:S(2)}) %collective-permute-start.1) | collective-permute-done | bytes 458784 | tf_op jit(solution)/shard_map/ppermute | solution.py:282
  52.2 1.3 convert_add_fusion.1
  53.4 0.0 copy-start.4
  53.5 0.9 copy-done.4
  54.4 1.7 %collective-permute-start.2 = (bf16[32,3584]{1,0:T(8,128)(2,1)S(1)}, bf16[32,3584]{1,0:T(8,128)(2,1)S(1)}, u32[]{:S(2)}, u32[]{:S(2)}) collective-permute-start(bf16[32,3584]{1,0:T(8,128)(2,1)S(1)} %dynamic-slice_convert_fusion.1), channel_id=1, source_target_pairs={{0,4},{1,5},{2,6},{3,7},{4,0},{5,1},{6,2},{7,3},{8,12},{9,13},{10,... | collective-permute-start | bytes 688136 | tf_op jit(solution)/shard_map/ppermute | solution.py:282
  56.1 0.0 copy-done
  56.1 15.4 %shard_map.112 = bf16[2000,3584]{1,0:T(8,128)(2,1)} custom-call(s32[1,256]{1,0:T(1,128)S(1)} %bitcast.36, bf16[2000,256]{1,0:T(8,128)(2,1)S(1)} %fusion.8.slope_ref, bf16[256,3584]{1,0:T(8,128)(2,1)S(1)} %fusion.2.normed_ref, bf16[256,3584]{1,0:T(8,128)(2,1)S(1)} %copy-done), custom_call_target="tpu_custom_call" | custom-call | flops 7340032000 | bytes 14336000 | tf_op jit(solution)/shard_map/pallas_call | solution.py:316
  71.5 0.0 copy-start.7
  71.5 0.0 collective-permute-done.2
  71.5 1.1 convert_add_fusion.2
  72.6 1.1 collective-permute-start.3
  73.7 0.8 dynamic-slice_convert_fusion.4.refs_2_
  74.5 2.9 %collective-permute-done.3 = bf16[16,3584]{1,0:T(8,128)(2,1)S(1)} collective-permute-done((bf16[16,3584]{1,0:T(8,128)(2,1)S(1)}, bf16[16,3584]{1,0:T(8,128)(2,1)S(1)}, u32[]{:S(2)}, u32[]{:S(2)}) %collective-permute-start.3) | collective-permute-done | bytes 114720 | tf_op jit(solution)/shard_map/ppermute | solution.py:282
  77.5 2.1 %collective-permute-start.4 = (bf16[8,3584]{1,0:T(8,128)(2,1)S(1)}, bf16[8,3584]{1,0:T(8,128)(2,1)S(1)}, u32[]{:S(2)}, u32[]{:S(2)}) collective-permute-start(bf16[8,3584]{1,0:T(8,128)(2,1)S(1)} %dynamic-slice_convert_fusion.3), channel_id=1, source_target_pairs={{0,16},{1,17},{2,18},{3,19},{4,20},{5,21},{6,22},{7,23},{8,24},{9,... | collective-permute-start | bytes 172040 | tf_op jit(solution)/shard_map/ppermute | solution.py:282
  79.6 0.0 copy-done.7
  79.6 0.6 convert_reduce_fusion
  81.6 1.7 %collective-permute-done.4 = bf16[8,3584]{1,0:T(8,128)(2,1)S(1)} collective-permute-done((bf16[8,3584]{1,0:T(8,128)(2,1)S(1)}, bf16[8,3584]{1,0:T(8,128)(2,1)S(1)}, u32[]{:S(2)}, u32[]{:S(2)}) %collective-permute-start.4) | collective-permute-done | bytes 57376 | tf_op jit(solution)/shard_map/ppermute | solution.py:282
  83.3 57.8 %shard_map.111 = (bf16[16,16,3584]{2,1,0:T(8,128)(2,1)S(1)}, bf16[16,16,3584]{2,1,0:T(8,128)(2,1)S(1)}, f32[32,128]{1,0:T(8,128)S(1)}) custom-call(f32[32,8,3584]{2,1,0:T(8,128)} %convolution_bitcast_fusion.refs_0_, f32[8,3584]{1,0:T(8,128)S(1)} %convert_add_fusion.4.refs_1_, f32[8,3584]{1,0:T(8,128)S(1)} %dynamic-slice_convert_fusion.4.refs_2_, ...), custom_call_target="tpu_custom_call" | custom-call | tf_op jit(solution)/shard_map/pallas_call | solution.py:245
  141.2 1.6 %multiply_convert_fusion = bf16[16,16,3584]{2,1,0:T(8,128)(2,1)} fusion(bf16[16,16,3584]{2,1,0:T(8,128)(2,1)S(1)} %get-tuple-element.8), kind=kLoop, calls=%fused_computation.7 | loop fusion | flops 2752512 | bytes 3670016 | tf_op jit(solution)/shard_map/convert_element_type | solution.py:384
  142.7 0.6 slice_bitcast_fusion
  143.3 1.2 copy.14
  (12 shorter events, 0.1 us)
Async XLA Ops:
  1.8 12.7 %copy-start.1 = (bf16[2000,3584]{1,0:T(8,128)(2,1)S(1)}, bf16[2000,3584]{1,0:T(8,128)(2,1)}, u32[]{:S(2)}) copy-start(bf16[2000,3584]{1,0:T(8,128)(2,1)} %param.13) | copy-start | bytes 43008004
  11.0 3.5 %copy-start.5 = (bf16[256,3584]{1,0:T(8,128)(2,1)}, bf16[256,3584]{1,0:T(8,128)(2,1)S(1)}, u32[]{:S(2)}) copy-start(bf16[256,3584]{1,0:T(8,128)(2,1)S(1)} %convolution_convert_fusion) | copy-start | bytes 5505028
  11.0 2.5 %copy-start.2 = (bf16[256,3584]{1,0:T(8,128)(2,1)S(1)}, bf16[256,3584]{1,0:T(8,128)(2,1)}, u32[]{:S(2)}) copy-start(bf16[256,3584]{1,0:T(8,128)(2,1)} %param.10) | copy-start | bytes 5505028
  11.0 2.9 %copy-start.6 = (f32[3584]{0:T(1024)S(1)}, f32[3584]{0:T(1024)}, u32[]{:S(2)}) copy-start(f32[3584]{0:T(1024)} %param.11) | copy-start | bytes 43012
  12.0 23.6 %collective-permute-start = (bf16[128,3584]{1,0:T(8,128)(2,1)}, bf16[128,3584]{1,0:T(8,128)(2,1)}, u32[]{:S(2)}, u32[]{:S(2)}) collective-permute-start(bf16[128,3584]{1,0:T(8,128)(2,1)} %constant_dynamic-slice_fusion), channel_id=1, source_target_pairs={{0,1},{1,0},{2,3},{3,2},{4,5},{5,4},{6,7},{7,6},{8,9},{9,8},{10,11... | collective-permute-start | bytes 2752520 | tf_op jit(solution)/shard_map/ppermute | solution.py:282
  13.9 0.7 copy-start.10
  14.6 6.0 %copy-start.9 = (s32[256]{0:T(256)S(1)}, s32[256]{0:T(256)}, u32[]{:S(2)}) copy-start(s32[256]{0:T(256)} %param.9) | copy-start | bytes 3076
  37.3 1.2 copy-start.3
  39.4 10.7 %copy-start.8 = (s32[256]{0:T(256)S(1)}, s32[256]{0:T(256)}, u32[]{:S(2)}) copy-start(s32[256]{0:T(256)} %param.7) | copy-start | bytes 3076
  39.4 12.8 %collective-permute-start.1 = (bf16[64,3584]{1,0:T(8,128)(2,1)}, bf16[64,3584]{1,0:T(8,128)(2,1)S(1)}, u32[]{:S(2)}, u32[]{:S(2)}) collective-permute-start(bf16[64,3584]{1,0:T(8,128)(2,1)} %dynamic-slice_convert_fusion), channel_id=1, source_target_pairs={{0,2},{1,3},{2,0},{3,1},{4,6},{5,7},{6,4},{7,5},{8,10},{9,11},{10,... | collective-permute-start | bytes 1376264 | tf_op jit(solution)/shard_map/ppermute | solution.py:282
  50.0 6.1 %copy-start = (bf16[256,3584]{1,0:T(8,128)(2,1)S(1)}, bf16[256,3584]{1,0:T(8,128)(2,1)}, u32[]{:S(2)}) copy-start(bf16[256,3584]{1,0:T(8,128)(2,1)} %cotangent_ref) | copy-start | bytes 5505028
  53.4 0.9 copy-start.4
  54.4 17.1 %collective-permute-start.2 = (bf16[32,3584]{1,0:T(8,128)(2,1)S(1)}, bf16[32,3584]{1,0:T(8,128)(2,1)S(1)}, u32[]{:S(2)}, u32[]{:S(2)}) collective-permute-start(bf16[32,3584]{1,0:T(8,128)(2,1)S(1)} %dynamic-slice_convert_fusion.1), channel_id=1, source_target_pairs={{0,4},{1,5},{2,6},{3,7},{4,0},{5,1},{6,2},{7,3},{8,12},{9,13},{10,... | collective-permute-start | bytes 688136 | tf_op jit(solution)/shard_map/ppermute | solution.py:282
  71.5 8.1 %copy-start.7 = (f32[4,128]{1,0:T(4,128)S(1)}, f32[4,128]{1,0:T(4,128)}, u32[]{:S(2)}) copy-start(f32[4,128]{1,0:T(4,128)} %shard_map.110) | copy-start | bytes 6148
  72.6 4.9 %collective-permute-start.3 = (bf16[16,3584]{1,0:T(8,128)(2,1)S(1)}, bf16[16,3584]{1,0:T(8,128)(2,1)S(1)}, u32[]{:S(2)}, u32[]{:S(2)}) collective-permute-start(bf16[16,3584]{1,0:T(8,128)(2,1)S(1)} %dynamic-slice_convert_fusion.2), channel_id=1, source_target_pairs={{0,8},{1,9},{2,10},{3,11},{4,12},{5,13},{6,14},{7,15},{8,0},{9,1},... | collective-permute-start | bytes 344072 | tf_op jit(solution)/shard_map/ppermute | solution.py:282
  77.5 5.8 %collective-permute-start.4 = (bf16[8,3584]{1,0:T(8,128)(2,1)S(1)}, bf16[8,3584]{1,0:T(8,128)(2,1)S(1)}, u32[]{:S(2)}, u32[]{:S(2)}) collective-permute-start(bf16[8,3584]{1,0:T(8,128)(2,1)S(1)} %dynamic-slice_convert_fusion.3), channel_id=1, source_target_pairs={{0,16},{1,17},{2,18},{3,19},{4,20},{5,21},{6,22},{7,23},{8,24},{9,... | collective-permute-start | bytes 172040 | tf_op jit(solution)/shard_map/ppermute | solution.py:282
